TPU v7x, 32 devices: a whole 2x2x4 slice. The times are simulated.
32 devices in a mesh: layer: 8 (over z, x), rep: 4 (over y, core).
Axes of the slice: x: 2, y: 2, z: 4, core: 2. Of those that a mesh axis runs over, the one named last changes fastest.
Arguments:
- inverse_root: bfloat16 [64, 16, 128, 128], P('layer', 'rep'), may hold values from -0.625 to 0.625
- square_root: bfloat16 [64, 16, 128, 128], P('layer', 'rep'), may hold values from -0.625 to 0.625
- pattern: int32 [64, 16], P('layer', 'rep'), may hold values from 0 to 1, as said below
Outputs:
- inverse_next: bfloat16 [64, 16, 128, 128], P('layer', 'rep')
- square_next: bfloat16 [64, 16, 128, 128], P('layer', 'rep')
Inputs may be any that keep to these rules, and one draw needn't show every extreme that they name: 1 marks a tile of the common pattern. Slot 8 is 1 in every block row, and slot w of block row i is 0 where i - 8 + w lies outside 0 to 63.
All inputs are finite; a program needn't handle non-finite values.
Results may differ from a plain program's by a relative error of at most 0.018.
Values may be sent and summed in bfloat16 or wider, within the bound.
A program may use at most 128 MiB of HBM per device.

v0:
```python
import functools

import jax
import jax.numpy as jnp
from jax import lax
from jax.experimental import pallas as pl
from jax.experimental.pallas import tpu as pltpu
from jax.sharding import PartitionSpec as P

MESH = pl.DeviceIdType.MESH
VMEM = pl.BlockSpec(memory_space=pltpu.VMEM)
SMEM = pl.BlockSpec(memory_space=pltpu.SMEM)
SEMAPHORES = 256


def reached(rows, band, low, high):
    half = band // 2
    found = {1: {}, -1: {}}
    for i in range(rows):
        for u in range(band):
            j = i - half + u
            if 0 <= j < rows:
                continue
            assert -rows <= j < 2 * rows
            side, a = (1, j + rows) if j < 0 else (-1, j - rows)
            for w in range(low, high):
                v = w + half - u
                if 0 <= v < band:
                    lo, hi = found[side].get(a, (v, v + 1))
                    found[side][a] = (min(lo, v), max(hi, v + 1))
    return found


def rectangles(spans, first, last):
    cut = []
    for a in sorted(spans):
        lo, hi = max(spans[a][0], first), min(spans[a][1], last)
        if lo >= hi:
            continue
        if cut and cut[-1][1] == a and cut[-1][2:] == (lo, hi):
            cut[-1] = (cut[-1][0], a + 1, lo, hi)
        else:
            cut.append((a, a + 1, lo, hi))
    return cut


class Later:
    def __init__(self, make, args=None):
        self.make, self.args = make, args

    def __call__(self, *args):
        return Later(self.make, args)

    def start(self):
        self.make(*self.args).start()

    def wait_recv(self):
        self.make(*self.args).wait_recv()

    def wait_send(self):
        self.make(*self.args).wait_send()


def step_kernel(layers, reps, refs_shape, pattern, z_own, y_own, z_next, y_next, y_wide, z_wide, u_wide, send_sems, recv_sems):
    rows, slots, tile = refs_shape
    band = slots * reps
    half = band // 2
    layer, rep = lax.axis_index("layer"), lax.axis_index("rep")
    after, before = lax.rem(layer + 1, layers), lax.rem(layer + layers - 1, layers)
    may_send = {1: layer + 1 < layers, -1: layer > 0}
    may_take = {1: layer > 0, -1: layer + 1 < layers}
    bits = []
    bit = reps // 2
    while bit >= 2:
        bits.append(bit)
        bit //= 2
    masks = list(range(0, reps, 2))
    keys = {}
    wides = {"y": y_wide, "z": z_wide, "u": u_wide}
    relayed = ("z", "u") if reps == 4 else ()

    def keep(i, _):
        for w in range(slots):
            good = pattern[i, w] == 1
            for own, wide in ((y_own, y_wide), (z_own, z_wide)):
                part = own[i, w]
                wide[rows + i, rep * slots + w] = jnp.where(good, part, jnp.zeros_like(part))
        return 0

    lax.fori_loop(0, rows, keep, 0)

    barrier = pltpu.get_barrier_semaphore()
    for place in (after, before):
        pl.semaphore_signal(barrier, inc=1, device_id={"layer": place}, device_id_type=MESH)
    for flip in [1] + bits:
        partner = rep + flip * (1 - 2 * lax.rem(lax.div(rep, flip), 2))
        pl.semaphore_signal(barrier, inc=1, device_id={"rep": partner}, device_id_type=MESH)
    pl.semaphore_wait(barrier, 3 + len(bits))

    def schedule(me):
        chip = me // 2
        remote = []
        need = reached(rows, band, chip * 2 * slots, (chip + 1) * 2 * slots)
        union = reached(rows, band, 0, band)
        other = reached(rows, band, (1 - chip) * 2 * slots, (2 - chip) * 2 * slots) if relayed else None
        direct_side = 1 if chip == 0 else -1

        def spans(s, side):
            if s not in relayed:
                return need[side]
            return union[side] if side == direct_side else {}

        def arriving(s, side):
            return spans(s, side) or need[side]

        def cut(which, q):
            return rectangles(which, q * slots, (q + 1) * slots)

        def base(side):
            return 0 if side == 1 else 2 * rows

        def copy(key, src, dst, device):
            n = keys.setdefault(key, len(keys))
            return pltpu.make_async_remote_copy(
                src_ref=src, dst_ref=dst, send_sem=send_sems.at[n], recv_sem=recv_sems.at[n],
                device_id=device, device_id_type=MESH,
            )

        def begin(guard, made):
            remote.append((guard, made))
            if guard is None:
                made.start()
            else:
                pl.when(guard)(made.start)

        def shard(s, q):
            return wides[s].at[pl.ds(rows, rows), pl.ds(q * slots, slots)]

        @Later
        def across(s, m, bit):
            part = shard(s, me ^ bit ^ m)
            return copy(("y", s, m), part, part, {"rep": me ^ bit})

        @Later
        def across_in(s, m, bit):
            part = shard(s, me ^ m)
            return copy(("y", s, m), part, part, {"rep": me ^ bit})

        @Later
        def to_core(s, m):
            part = shard(s, me ^ m)
            return copy(("d", s, m), part, part, {"rep": me ^ 1})

        @Later
        def to_core_in(s, m):
            part = shard(s, me ^ 1 ^ m)
            return copy(("d", s, m), part, part, {"rep": me ^ 1})

        @Later
        def to_layer(s, side, m, k, piece):
            a, b, lo, hi = piece
            src = wides[s].at[pl.ds(rows + a, b - a), pl.ds(lo, hi - lo)]
            dst = wides[s].at[pl.ds(base(side) + a, b - a), pl.ds(lo, hi - lo)]
            return copy(("x", s, side, m, k), src, dst, {"layer": after if side == 1 else before})

        @Later
        def relay(s, side, m, k, piece):
            a, b, lo, hi = piece
            part = wides[s].at[pl.ds(base(side) + a, b - a), pl.ds(lo, hi - lo)]
            return copy(("r", s, side, m, k), part, part, {"rep": me ^ 2})

        @Later
        def halo_to_core(s, side, m, q):
            pieces = cut(arriving(s, side), q)
            a, b = min(c[0] for c in pieces), max(c[1] for c in pieces)
            part = wides[s].at[pl.ds(base(side) + a, b - a), pl.ds(q * slots, slots)]
            return copy(("h", s, side, m), part, part, {"rep": me ^ 1})

        def send_layer(s, m):
            for side in (1, -1):
                for k, piece in enumerate(cut(spans(s, side), me ^ m)):
                    begin(may_send[side], to_layer(s, side, m, k, piece))

        def take_direct(s, m):
            for side in (1, -1):
                pieces = cut(spans(s, side), me ^ m)
                if pieces:
                    made = [to_layer(s, side, m, k, piece) for k, piece in enumerate(pieces)]
                    onward = [halo_to_core(s, side, m, me ^ m)]
                    if s in relayed:
                        onward += [
                            relay(s, side, m ^ 2, k, piece)
                            for k, piece in enumerate(cut(other[side], me ^ m))
                        ]
                    pass_on(side, made, onward)

        def take_relayed(s, m):
            for side in (1, -1):
                if s in relayed and side != direct_side:
                    pieces = cut(need[side], me ^ m)
                    if pieces:
                        made = [relay(s, side, m, k, piece) for k, piece in enumerate(pieces)]
                        pass_on(side, made, [halo_to_core(s, side, m, me ^ m)])

        def pass_on(side, made, onward):
            remote.extend((may_take[side], o) for o in onward)

            @pl.when(may_take[side])
            def _():
                for one in made:
                    one.wait_recv()
                for one in onward:
                    one.start()

        def start_gather(s):
            if bits:
                begin(None, across(s, bits[0], bits[0]))
            begin(None, to_core(s, 0))

        def gather(s, halo):
            held = [0]
            for n, bit in enumerate(bits):
                if n > 0:
                    for m in held:
                        begin(None, across(s, m ^ bit, bit))
                fresh = [m ^ bit for m in held]
                for m in fresh:
                    across_in(s, m, bit).wait_recv()
                    begin(None, to_core(s, m))
                    if halo:
                        send_layer(s, m)
                held = held + fresh

        def finish_own(s):
            for m in masks:
                to_core_in(s, m).wait_recv()

        def finish_halo(s):
            for side in (1, -1):
                made = [
                    halo_to_core(s, side, m, me ^ 1 ^ m)
                    for m in masks
                    if cut(arriving(s, side), me ^ 1 ^ m)
                ]

                @pl.when(may_take[side])
                def _():
                    for one in made:
                        one.wait_recv()

        start_gather("y")
        start_gather("z")
        send_layer("y", 0)
        gather("y", True)
        send_layer("z", 0)
        take_direct("y", 0)
        gather("z", True)
        for m in masks[1:]:
            take_direct("y", m)
        for s in ("y", "z"):
            finish_own(s)
        finish_halo("y")
        yield
        start_gather("u")
        send_layer("u", 0)
        for m in masks:
            take_direct("z", m)
        gather("u", True)
        for m in masks:
            take_relayed("z", m)
        finish_own("u")
        finish_halo("z")
        yield
        for m in masks:
            take_direct("u", m)
        for m in masks:
            take_relayed("u", m)
        finish_halo("u")
        yield
        for guard, made in remote:
            if guard is None:
                made.wait_send()
            else:
                pl.when(guard)(made.wait_send)
        yield

    plans = [schedule(me) for me in range(reps)]

    def advance():
        for me in range(reps):
            pl.when(rep == me)(functools.partial(next, plans[me]))

    down = lax.broadcasted_iota(jnp.int32, (tile, tile), 0)
    right = lax.broadcasted_iota(jnp.int32, (tile, tile), 1)
    identity = jnp.where(down == right, 1.5, 0.0).astype(jnp.float32)

    def multiply(left, right, store):
        def step(i, _):
            total = product_row(i, left, right, layer, rep, layers, rows, slots, band)
            for w in range(slots):
                store(i, w, pattern[i, w] == 1, total[:, w * tile : (w + 1) * tile])
            return 0

        lax.fori_loop(0, rows, step, 0)

    def store_update(i, w, good, value):
        value = -0.5 * value + jnp.where(rep * slots + w == half, identity, 0.0)
        u_wide[rows + i, rep * slots + w] = jnp.where(good, value, 0.0).astype(jnp.bfloat16)

    def store_inverse(i, w, good, value):
        z_next[i, w] = jnp.where(good, value, 0.0).astype(jnp.bfloat16)

    def store_square(i, w, good, value):
        y_next[i, w] = jnp.where(good, value, 0.0).astype(jnp.bfloat16)

    advance()
    multiply(z_wide, y_wide, store_update)
    advance()
    multiply(u_wide, z_wide, store_inverse)
    advance()
    multiply(y_wide, u_wide, store_square)
    advance()
    assert len(keys) <= send_sems.shape[0]


def product_row(i, left, right, layer, rep, layers, rows, slots, band):
    half = band // 2
    step = 4
    total = None
    for first in range(0, band, step):
        wide = jnp.concatenate([left[rows + i, u] for u in range(first, first + step)], axis=1)
        tall = []
        for u in range(first, first + step):
            row = layer * rows + i - half + u
            inside = jnp.logical_and(row >= 0, row < layers * rows)
            tiles = []
            for w in range(slots):
                v = rep * slots + w + half - u
                good = jnp.logical_and(inside, jnp.logical_and(v >= 0, v < band))
                part = right[i + u + rows - half, lax.rem(v + band, band)]
                tiles.append(jnp.where(good, part, jnp.zeros_like(part)))
            tall.append(jnp.concatenate(tiles, axis=1))
        piece = jnp.dot(wide, jnp.concatenate(tall, axis=0), preferred_element_type=jnp.float32)
        total = piece if total is None else total + piece
    return total


def solution(mesh):
    layers, reps = mesh.shape["layer"], mesh.shape["rep"]

    def body(inverse_root, square_root, pattern):
        rows, slots = pattern.shape
        tile = inverse_root.shape[2:]
        local = jax.ShapeDtypeStruct((rows, slots) + tile, jnp.bfloat16)
        wide = pltpu.VMEM((3 * rows, slots * reps) + tile, jnp.bfloat16)
        return pl.pallas_call(
            functools.partial(step_kernel, layers, reps, (rows, slots, tile[0])),
            out_shape=(local, local),
            in_specs=[SMEM, VMEM, VMEM],
            out_specs=(VMEM, VMEM),
            scratch_shapes=[
                wide,
                wide,
                wide,
                pltpu.SemaphoreType.DMA((SEMAPHORES,)),
                pltpu.SemaphoreType.DMA((SEMAPHORES,)),
            ],
            compiler_params=pltpu.CompilerParams(
                collective_id=0, has_side_effects=True, vmem_limit_bytes=60 * 1024 * 1024
            ),
            name="newton_step",
        )(pattern, inverse_root, square_root)

    placed = P("layer", "rep", None, None)
    return jax.shard_map(
        body,
        mesh=mesh,
        in_specs=(placed, placed, P("layer", "rep")),
        out_specs=(placed, placed),
        check_vma=False,
    )
```

profile of v0, /device:TPU:6, one launch (start us, length us, event | category | flops | bytes accessed | tf_op | source)
XLA Modules:
  0.0 144.6 jit_solution(17228904135822850604)
XLA Ops:
  0.6 1.3 copy.5.pattern
  2.0 139.2 %newton_step.1 = (bf16[8,4,128,128]{3,2,1,0:T(8,128)(2,1)}, bf16[8,4,128,128]{3,2,1,0:T(8,128)(2,1)}) custom-call(s32[8,4]{1,0:T(8,128)} %copy.5.pattern, bf16[8,4,128,128]{3,2,1,0:T(8,128)(2,1)} %z_own.1, bf16[8,4,128,128]{3,2,1,0:T(8,128)(2,1)} %y_own.1), custom_call_target="tpu_custom_call" | custom-call | tf_op jit(solution)/shard_map/newton_step/pallas_call | solution.py:356
  141.2 0.0 copy-start
  141.2 2.4 %copy.8 = bf16[8,4,128,128]{3,2,1,0:T(8,128)(2,1)} copy(bf16[8,4,128,128]{3,2,1,0:T(8,128)(2,1)} %get-tuple-element.4) | data formatting | bytes 2097152
  143.6 0.0 copy-done
  143.6 1.0 copy.9
Async XLA Ops:
  141.2 2.4 %copy-start = (bf16[8,4,128,128]{3,2,1,0:T(8,128)(2,1)S(1)}, bf16[8,4,128,128]{3,2,1,0:T(8,128)(2,1)}, u32[]{:S(2)}) copy-start(bf16[8,4,128,128]{3,2,1,0:T(8,128)(2,1)} %get-tuple-element.5) | copy-start | bytes 3145732
where the time goes:
time: 145 us
  Pallas kernels  139 us (96%)
  local copies, waits for them, and re-layouts  4.72 us (3%)
    pallas_call x1, Pallas kernels, body(): pl.pallas_call(functools.partial(step_kernel, layers, reps, (rows, slots,...  139 us
    unnamed x5, local copies, waits for them, and re-layouts  4.72 us

commit v1 on v0

--- a/solution.py
+++ b/solution.py
@@ -345,6 +345,439 @@
     return total
 
 
+PAIRED_SEMAPHORES = 208
+
+
+def block_spans(rows, band):
+    lower = {a: (0, band // 2 - a) for a in range(rows)}
+    upper = {a: (band - a, band) for a in range(1, rows)}
+    return lower, upper
+
+
+def paired_kernel(
+    layers, reps, refs_shape, pattern, z_own, y_own, z_next, y_next,
+    y_wide, z_wide, u_wide, z_sum, y_sum, z_out, y_out, z_in, y_in, send_sems, recv_sems,
+):
+    rows, slots, tile = refs_shape
+    band = slots * reps
+    half = band // 2
+    step = 2
+    chunks = [(a, a + step) for a in range(0, rows, step)]
+    layer, rep = lax.axis_index("layer"), lax.axis_index("rep")
+    after, before = lax.rem(layer + 1, layers), lax.rem(layer + layers - 1, layers)
+    may_send = {1: layer + 1 < layers, -1: layer > 0}
+    may_take = {1: layer > 0, -1: layer + 1 < layers}
+    wides = {"y": y_wide, "z": z_wide, "u": u_wide}
+    lower, upper = block_spans(rows, band)
+    keys = {}
+
+    barrier = pltpu.get_barrier_semaphore()
+    for place in (after, before):
+        pl.semaphore_signal(barrier, inc=1, device_id={"layer": place}, device_id_type=MESH)
+    for flip in (1, 2):
+        partner = rep + flip * (1 - 2 * lax.rem(lax.div(rep, flip), 2))
+        pl.semaphore_signal(barrier, inc=1, device_id={"rep": partner}, device_id_type=MESH)
+
+    def keep(own, wide):
+        def row(i, _):
+            for w in range(slots):
+                part = own[i, w]
+                wide[rows + i, rep * slots + w] = jnp.where(pattern[i, w] == 1, part, jnp.zeros_like(part))
+            return 0
+
+        lax.fori_loop(0, rows, row, 0)
+
+    def schedule(me):
+        chip = me // 2
+        remote = []
+
+        def base(side):
+            return 0 if side == 1 else 2 * rows
+
+        def own_side(who):
+            return -1 if who // 2 == 0 else 1
+
+        def own_spans(who):
+            return lower if who // 2 == 0 else upper
+
+        def cut(spans, q, chunk):
+            kept = {a: spans[a] for a in spans if chunk[0] <= a < chunk[1]}
+            return rectangles(kept, q * slots, (q + 1) * slots)
+
+        def needs(who, side):
+            low = who // 2 * 2 * slots
+            return reached(rows, band, low, low + 2 * slots)[side]
+
+        def sent(s, who, side, n):
+            if s == "y":
+                return needs(who, side)
+            return own_spans(who) if n == 0 and side == own_side(who) else {}
+
+        def extra(who):
+            if who // 2:
+                return {}
+            need = needs(who, -1)
+            return {a: (need[a][1] if a in need else 0, lower[a][1]) for a in lower}
+
+        def relayed(who):
+            side = own_side(who)
+            need, have = needs(who ^ 2, side), own_spans(who)
+            found = {}
+            for a in have:
+                if a in need:
+                    lo, hi = max(need[a][0], have[a][0]), min(need[a][1], have[a][1])
+                    if lo < hi:
+                        found[a] = (lo, hi)
+            return found
+
+        def copy(key, src, dst, device):
+            n = keys.setdefault(key, len(keys))
+            return lambda: pltpu.make_async_remote_copy(
+                src_ref=src, dst_ref=dst, send_sem=send_sems.at[0], recv_sem=recv_sems.at[n],
+                device_id=device, device_id_type=MESH,
+            )
+
+        def begin(guard, made):
+            if not made:
+                return
+            remote.append((guard, made))
+
+            def go():
+                for one in made:
+                    one().start()
+
+            go() if guard is None else pl.when(guard)(go)
+
+        def take(guard, made, onward=()):
+            if not made:
+                return
+            remote.append((guard, list(onward)))
+
+            def go():
+                for one in made:
+                    one().wait_recv()
+                for one in onward:
+                    one().start()
+
+            go() if guard is None else pl.when(guard)(go)
+
+        def shard(s, q, chunk):
+            return wides[s].at[pl.ds(rows + chunk[0], chunk[1] - chunk[0]), pl.ds(q * slots, slots)]
+
+        def swap(s, q, chunk):
+            part = shard(s, q, chunk)
+            return copy(("swap", s, chunk), part, part, {"rep": me ^ 2})
+
+        def pair(s, q, chunk):
+            part = shard(s, q, chunk)
+            return copy(("pair", s, chunk), part, part, {"rep": me ^ 1})
+
+        def pass_pair(s, q, chunk):
+            part = shard(s, q, chunk)
+            return copy(("pass", s, chunk), part, part, {"rep": me ^ 1})
+
+        def boxes(name, s, side, n, chunk, pieces, device, start):
+            made = []
+            for k, (a, b, lo, hi) in enumerate(pieces):
+                src = wides[s].at[pl.ds(start + a, b - a), pl.ds(lo, hi - lo)]
+                dst = wides[s].at[pl.ds(base(side) + a, b - a), pl.ds(lo, hi - lo)]
+                made.append(copy((name, s, side, n, chunk, k), src, dst, device))
+            return made
+
+        def group(who, n):
+            return who ^ 2 if n else who
+
+        def to_layer(s, side, n, chunk):
+            pieces = cut(sent(s, me, side, n), group(me, n), chunk)
+            return boxes("x", s, side, n, chunk, pieces, {"layer": after if side == 1 else before}, rows)
+
+        def layer_pass(s, side, n, chunk, who):
+            pieces = cut(sent(s, who, side, n), group(who, n), chunk)
+            return boxes("xp", s, side, n, chunk, pieces, {"rep": me ^ 1}, base(side))
+
+        def extra_to_layer():
+            return boxes("e", "y", -1, 0, 0, cut(extra(me), me, (0, rows)), {"layer": before}, rows)
+
+        def extra_pass(who):
+            return boxes("ep", "y", -1, 0, 0, cut(extra(who), who, (0, rows)), {"rep": me ^ 1}, 2 * rows)
+
+        def relay(s, chunk, who):
+            pieces = cut(relayed(who), who, chunk)
+            side = own_side(who)
+            return boxes("r", s, side, 0, chunk, pieces, {"rep": me ^ 2}, base(side))
+
+        def relay_pass(s, chunk, who):
+            pieces = cut(relayed(who), who, chunk)
+            side = own_side(who)
+            return boxes("rp", s, side, 0, chunk, pieces, {"rep": me ^ 1}, base(side))
+
+        def partial_out(s, chunk):
+            source, target = (z_out, z_in) if s == "z" else (y_out, y_in)
+            made = []
+            for k, (a, b, lo, hi) in enumerate(cut(own_spans(me), me, chunk)):
+                at = (pl.ds(a, b - a), pl.ds(lo - me * slots, hi - lo))
+                place = after if chip == 0 else before
+                made.append(copy(("p", s, chunk, k), source.at[at], target.at[at], {"layer": place}))
+            return made
+
+        def start_swap(s, chunk):
+            begin(None, [swap(s, me, chunk)])
+
+        def start_pair(s, chunk):
+            begin(None, [pair(s, me, chunk)])
+
+        def end_swap(s, chunk):
+            take(None, [swap(s, me ^ 2, chunk)], [pass_pair(s, me ^ 2, chunk)])
+
+        def send_layer(s, n, chunk):
+            for side in (1, -1):
+                begin(may_send[side], to_layer(s, side, n, chunk))
+
+        def take_layer(s, n, chunk):
+            for side in (1, -1):
+                onward = layer_pass(s, side, n, chunk, me)
+                if s != "y":
+                    onward = onward + relay(s, chunk, me)
+                take(may_take[side], to_layer(s, side, n, chunk), onward)
+
+        def take_layer_pass(s, n, chunk):
+            for side in (1, -1):
+                take(may_take[side], layer_pass(s, side, n, chunk, me ^ 1))
+
+        def take_relay(s, chunk):
+            take(may_take[own_side(me ^ 2)], relay(s, chunk, me ^ 2), relay_pass(s, chunk, me ^ 2))
+
+        def take_relay_pass(s, chunk):
+            take(may_take[own_side(me ^ 2)], relay_pass(s, chunk, me ^ 3))
+
+        out_side = 1 if chip == 0 else -1
+
+        for chunk in chunks:
+            start_swap("y", chunk)
+            send_layer("y", 0, chunk)
+        for chunk in chunks:
+            start_pair("y", chunk)
+        yield
+        for chunk in chunks:
+            start_swap("z", chunk)
+        for chunk in chunks:
+            start_pair("z", chunk)
+        for chunk in chunks:
+            end_swap("y", chunk)
+            send_layer("y", 1, chunk)
+        for n, chunk in enumerate(chunks):
+            take_layer("y", 0, chunk)
+        for n, chunk in enumerate(chunks):
+            end_swap("z", chunk)
+            take_layer("y", 1, chunk)
+        for chunk in chunks:
+            take(None, [pair("y", me ^ 1, chunk)])
+            take(None, [pass_pair("y", me ^ 3, chunk)])
+            take(None, [pair("z", me ^ 1, chunk)])
+            for n in (0, 1):
+                take_layer_pass("y", n, chunk)
+        begin(may_send[-1], extra_to_layer())
+        for chunk in chunks:
+            send_layer("z", 0, chunk)
+        for chunk in chunks:
+            take(None, [pass_pair("z", me ^ 3, chunk)])
+            yield
+            start_swap("u", chunk)
+            start_pair("u", chunk)
+            send_layer("u", 0, chunk)
+        take(may_take[-1], extra_to_layer(), extra_pass(me))
+        for n, chunk in enumerate(chunks):
+            take_layer("z", 0, chunk)
+            end_swap("u", chunk)
+            take(None, [pair("u", me ^ 1, chunk)])
+            take(None, [pass_pair("u", me ^ 3, chunk)])
+            yield
+        take(may_take[-1], extra_pass(me ^ 1))
+        for chunk in chunks[: len(chunks) // 2]:
+            take_layer("u", 0, chunk)
+        for chunk in chunks[: len(chunks) // 2]:
+            take_layer_pass("u", 0, chunk)
+        yield
+        for chunk in chunks[: len(chunks) // 2]:
+            begin(may_send[out_side], partial_out("z", chunk))
+        for chunk in chunks[len(chunks) // 2 :]:
+            take_layer("u", 0, chunk)
+        for chunk in chunks[len(chunks) // 2 :]:
+            take_layer_pass("u", 0, chunk)
+        yield
+        for chunk in chunks[len(chunks) // 2 :]:
+            begin(may_send[out_side], partial_out("z", chunk))
+        yield
+        for chunk in chunks:
+            begin(may_send[out_side], partial_out("y", chunk))
+        for chunk in chunks:
+            take_relay("z", chunk)
+        yield
+        for chunk in chunks:
+            take_layer_pass("z", 0, chunk)
+            take_relay("u", chunk)
+        for chunk in chunks:
+            take_relay_pass("z", chunk)
+            take_relay_pass("u", chunk)
+        yield
+        for chunk in chunks:
+            take(may_take[out_side], partial_out("z", chunk))
+        yield
+        for chunk in chunks:
+            take(may_take[out_side], partial_out("y", chunk))
+        yield
+        for guard, made in remote:
+
+            def end(made=made):
+                for one in made:
+                    one().wait_send()
+
+            if made:
+                end() if guard is None else pl.when(guard)(end)
+        yield
+
+    plans = [schedule(me) for me in range(reps)]
+
+    def advance():
+        for me in range(reps):
+            pl.when(rep == me)(functools.partial(next, plans[me]))
+
+    down = lax.broadcasted_iota(jnp.int32, (tile, tile), 0)
+    right_at = lax.broadcasted_iota(jnp.int32, (tile, tile), 1)
+    identity = jnp.where(down == right_at, 1.5, 0.0).astype(jnp.float32)
+    zero = jnp.zeros((tile, tile), jnp.bfloat16)
+
+    def multiply(lefts, rights):
+        wide = jnp.concatenate(lefts, axis=1)
+        tall = jnp.concatenate([jnp.concatenate(one, axis=1) for one in rights], axis=0)
+        return jnp.dot(wide, tall, preferred_element_type=jnp.float32)
+
+    def own_part(i, left, right):
+        lefts, rights = [], []
+        for t in range(rows):
+            u = half - i + t
+            lefts.append(left[rows + i, u])
+            line = []
+            for w in range(slots):
+                v = rep * slots + w + i - t
+                good = jnp.logical_and(v >= 0, v < band)
+                line.append(jnp.where(good, right[rows + t, lax.rem(v + band, band)], zero))
+            rights.append(line)
+        return multiply(lefts, rights)
+
+    def halo_part(i, left, right, inner):
+        lefts, rights = [], []
+        for t in range(rows):
+            u = lax.rem(t - i + band, band)
+            lefts.append(left[rows + i, u])
+            line = []
+            row = layer * rows + i - half + u
+            inside = jnp.logical_and(row >= 0, row < layers * rows)
+            for w in range(slots):
+                v = rep * slots + w + half - u
+                good = jnp.logical_and(inside, jnp.logical_and(v >= 0, v < band))
+                if inner:
+                    k = i - half + rep * slots + w
+                    good = jnp.logical_and(good, jnp.logical_and(k >= 0, k < rows))
+                line.append(jnp.where(good, right[i + u, lax.rem(v + band, band)], zero))
+            rights.append(line)
+        return multiply(lefts, rights)
+
+    def split(total, w):
+        return total[:, w * tile : (w + 1) * tile]
+
+    def update_rows(chunk):
+        def row(i, _):
+            total = own_part(i, z_wide, y_wide) + halo_part(i, z_wide, y_wide, False)
+            for w in range(slots):
+                value = -0.5 * split(total, w) + jnp.where(rep * slots + w == half, identity, 0.0)
+                value = jnp.where(pattern[i, w] == 1, value, 0.0)
+                u_wide[rows + i, rep * slots + w] = value.astype(jnp.bfloat16)
+            return 0
+
+        lax.fori_loop(chunk[0], chunk[1], row, 0)
+
+    def own_rows(left, right, total, chunk):
+        def row(i, _):
+            value = own_part(i, left, right)
+            for w in range(slots):
+                total[i, w] = split(value, w)
+            return 0
+
+        lax.fori_loop(chunk[0], chunk[1], row, 0)
+
+    def halo_rows(left, right, total):
+        def row(i, _):
+            value = halo_part(i, left, right, True)
+            for w in range(slots):
+                total[i, w] += split(value, w)
+            return 0
+
+        lax.fori_loop(0, rows, row, 0)
+
+    def partial_rows(left, right, out, chunk):
+        chip = lax.div(rep, 2)
+
+        def row(i, _):
+            lefts, rights = [], []
+            for t in range(rows):
+                u = t + half * chip
+                part = left[2 * rows * (1 - chip) + i, u]
+                lefts.append(jnp.where(lax.div(i + t, rows) == chip, part, zero))
+                j = lax.rem(i + t, rows)
+                rights.append([
+                    right[rows + j, rep * slots + w + half - u] for w in range(slots)
+                ])
+            value = multiply(lefts, rights)
+            for w in range(slots):
+                out[i, w] = split(value, w).astype(jnp.bfloat16)
+            return 0
+
+        lax.fori_loop(chunk[0], chunk[1], row, 0)
+
+    def finish(total, part, result):
+        def row(i, _):
+            for w in range(slots):
+                k = i - half + rep * slots + w
+                below = jnp.logical_and(k < 0, layer > 0)
+                above = jnp.logical_and(k >= rows, layer + 1 < layers)
+                more = jnp.where(jnp.logical_or(below, above), part[i, w].astype(jnp.float32), 0.0)
+                value = jnp.where(pattern[i, w] == 1, total[i, w] + more, 0.0)
+                result[i, w] = value.astype(jnp.bfloat16)
+            return 0
+
+        lax.fori_loop(0, rows, row, 0)
+
+    keep(y_own, y_wide)
+    pl.semaphore_wait(barrier, 4)
+    advance()
+    keep(z_own, z_wide)
+    for chunk in chunks:
+        advance()
+        update_rows(chunk)
+    for chunk in chunks:
+        advance()
+        own_rows(u_wide, z_wide, z_sum, chunk)
+    advance()
+    middle = rows // 2
+    partial_rows(u_wide, z_wide, z_out, (0, middle))
+    advance()
+    partial_rows(u_wide, z_wide, z_out, (middle, rows))
+    advance()
+    partial_rows(y_wide, u_wide, y_out, (0, rows))
+    advance()
+    own_rows(y_wide, u_wide, y_sum, (0, rows))
+    advance()
+    halo_rows(u_wide, z_wide, z_sum)
+    halo_rows(y_wide, u_wide, y_sum)
+    advance()
+    finish(z_sum, z_in, z_next)
+    advance()
+    finish(y_sum, y_in, y_next)
+    advance()
+    assert len(keys) <= recv_sems.shape[0]
+
+
 def solution(mesh):
     layers, reps = mesh.shape["layer"], mesh.shape["rep"]
 
@@ -353,18 +786,20 @@
         tile = inverse_root.shape[2:]
         local = jax.ShapeDtypeStruct((rows, slots) + tile, jnp.bfloat16)
         wide = pltpu.VMEM((3 * rows, slots * reps) + tile, jnp.bfloat16)
+        sems = [pltpu.SemaphoreType.DMA((SEMAPHORES,))] * 2
+        paired = reps == 4 and 2 * rows == slots * reps and rows % 4 == 0
+        kernel, extra = step_kernel, []
+        if paired:
+            kernel = paired_kernel
+            extra = [pltpu.VMEM((rows, slots) + tile, jnp.float32)] * 2
+            extra += [pltpu.VMEM((rows, slots) + tile, jnp.bfloat16)] * 4
+            sems = [pltpu.SemaphoreType.DMA((1,)), pltpu.SemaphoreType.DMA((PAIRED_SEMAPHORES,))]
         return pl.pallas_call(
-            functools.partial(step_kernel, layers, reps, (rows, slots, tile[0])),
+            functools.partial(kernel, layers, reps, (rows, slots, tile[0])),
             out_shape=(local, local),
             in_specs=[SMEM, VMEM, VMEM],
             out_specs=(VMEM, VMEM),
-            scratch_shapes=[
-                wide,
-                wide,
-                wide,
-                pltpu.SemaphoreType.DMA((SEMAPHORES,)),
-                pltpu.SemaphoreType.DMA((SEMAPHORES,)),
-            ],
+            scratch_shapes=[wide, wide, wide] + extra + sems,
             compiler_params=pltpu.CompilerParams(
                 collective_id=0, has_side_effects=True, vmem_limit_bytes=60 * 1024 * 1024
             ),

time: 145 us -> 120 us (0.83)
  the two profiles are of different devices: /device:TPU:6 before, /device:TPU:2 now
where the time goes in v1:
time: 120 us
  Pallas kernels  114 us (95%)
  local copies, waits for them, and re-layouts  4.72 us (4%)
    pallas_call x1, Pallas kernels, body(): pl.pallas_call(functools.partial(kernel, layers, reps, (rows, slots, tile...  114 us
    unnamed x5, local copies, waits for them, and re-layouts  4.72 us

profile of v1, /device:TPU:2, one launch (start us, length us, event | category | flops | bytes accessed | tf_op | source)
XLA Modules:
  0.0 119.8 jit_solution(10675982971755913025)
XLA Ops:
  0.6 1.3 %copy.5.pattern = s32[8,4]{1,0:T(8,128)} copy(s32[8,4]{0,1:T(4,128)} %param.5) | data formatting | bytes 256 | tf_op args[2]
  2.0 114.4 %newton_step.1 = (bf16[8,4,128,128]{3,2,1,0:T(8,128)(2,1)}, bf16[8,4,128,128]{3,2,1,0:T(8,128)(2,1)}) custom-call(s32[8,4]{1,0:T(8,128)} %copy.5.pattern, bf16[8,4,128,128]{3,2,1,0:T(8,128)(2,1)} %z_own.1, bf16[8,4,128,128]{3,2,1,0:T(8,128)(2,1)} %y_own.1), custom_call_target="tpu_custom_call" | custom-call | tf_op jit(solution)/shard_map/newton_step/pallas_call | solution.py:797
  116.4 0.0 copy-start
  116.4 2.4 %copy.8 = bf16[8,4,128,128]{3,2,1,0:T(8,128)(2,1)} copy(bf16[8,4,128,128]{3,2,1,0:T(8,128)(2,1)} %get-tuple-element.4) | data formatting | bytes 2097152
  118.8 0.0 copy-done
  118.8 1.0 copy.9
Async XLA Ops:
  116.4 2.4 %copy-start = (bf16[8,4,128,128]{3,2,1,0:T(8,128)(2,1)S(1)}, bf16[8,4,128,128]{3,2,1,0:T(8,128)(2,1)}, u32[]{:S(2)}) copy-start(bf16[8,4,128,128]{3,2,1,0:T(8,128)(2,1)} %get-tuple-element.5) | copy-start | bytes 3145732

commit v2 on v1

--- a/solution.py
+++ b/solution.py
@@ -345,7 +345,8 @@
     return total
 
 
-PAIRED_SEMAPHORES = 208
+PAIRED_SEMAPHORES = 144
+VMEM_BYTES = 52 * 1024 * 1024
 
 
 def block_spans(rows, band):
@@ -356,7 +357,7 @@
 
 def paired_kernel(
     layers, reps, refs_shape, pattern, z_own, y_own, z_next, y_next,
-    y_wide, z_wide, u_wide, z_sum, y_sum, z_out, y_out, z_in, y_in, send_sems, recv_sems,
+    y_wide, z_wide, u_wide, z_sum, y_sum, c_out, z_out, y_out, c_in, z_in, y_in, send_sems, recv_sems,
 ):
     rows, slots, tile = refs_shape
     band = slots * reps
@@ -368,6 +369,7 @@
     may_send = {1: layer + 1 < layers, -1: layer > 0}
     may_take = {1: layer > 0, -1: layer + 1 < layers}
     wides = {"y": y_wide, "z": z_wide, "u": u_wide}
+    partials = {"c": (c_out, c_in), "z": (z_out, z_in), "y": (y_out, y_in)}
     lower, upper = block_spans(rows, band)
     keys = {}
 
@@ -387,6 +389,33 @@
 
         lax.fori_loop(0, rows, row, 0)
 
+    class Parcel:
+        def __init__(self, n, pairs, device):
+            self.n, self.pairs, self.device = n, pairs, device
+
+        def copies(self):
+            for src, dst in self.pairs:
+                yield pltpu.make_async_remote_copy(
+                    src_ref=src, dst_ref=dst, send_sem=send_sems.at[0], recv_sem=recv_sems.at[self.n],
+                    device_id=self.device, device_id_type=MESH,
+                )
+
+        def start(self):
+            for one in self.copies():
+                one.start()
+
+        def wait_send(self):
+            for one in self.copies():
+                one.wait_send()
+
+        def wait_recv(self):
+            if len(self.pairs) == 1:
+                next(self.copies()).wait_recv()
+                return
+            tiles = sum(dst.shape[0] * dst.shape[1] for _, dst in self.pairs)
+            at = y_wide.at[pl.ds(0, 1), pl.ds(0, tiles)]
+            Parcel(self.n, [(at, at)], self.device).wait_recv()
+
     def schedule(me):
         chip = me // 2
         remote = []
@@ -409,17 +438,11 @@
             return reached(rows, band, low, low + 2 * slots)[side]
 
         def sent(s, who, side, n):
-            if s == "y":
-                return needs(who, side)
-            return own_spans(who) if n == 0 and side == own_side(who) else {}
-
-        def extra(who):
-            if who // 2:
-                return {}
-            need = needs(who, -1)
-            return {a: (need[a][1] if a in need else 0, lower[a][1]) for a in lower}
-
-        def relayed(who):
+            if side == own_side(who):
+                return {} if n else own_spans(who)
+            return shared(who ^ 2) if n and s == "y" else {}
+
+        def shared(who):
             side = own_side(who)
             need, have = needs(who ^ 2, side), own_spans(who)
             found = {}
@@ -431,11 +454,7 @@
             return found
 
         def copy(key, src, dst, device):
-            n = keys.setdefault(key, len(keys))
-            return lambda: pltpu.make_async_remote_copy(
-                src_ref=src, dst_ref=dst, send_sem=send_sems.at[0], recv_sem=recv_sems.at[n],
-                device_id=device, device_id_type=MESH,
-            )
+            return Parcel(keys.setdefault(key, len(keys)), [(src, dst)], device)
 
         def begin(guard, made):
             if not made:
@@ -444,7 +463,7 @@
 
             def go():
                 for one in made:
-                    one().start()
+                    one.start()
 
             go() if guard is None else pl.when(guard)(go)
 
@@ -455,9 +474,9 @@
 
             def go():
                 for one in made:
-                    one().wait_recv()
+                    one.wait_recv()
                 for one in onward:
-                    one().start()
+                    one.start()
 
             go() if guard is None else pl.when(guard)(go)
 
@@ -476,13 +495,16 @@
             part = shard(s, q, chunk)
             return copy(("pass", s, chunk), part, part, {"rep": me ^ 1})
 
+        def parcel(key, pairs, device):
+            return [Parcel(keys.setdefault(key, len(keys)), pairs, device)] if pairs else []
+
         def boxes(name, s, side, n, chunk, pieces, device, start):
-            made = []
-            for k, (a, b, lo, hi) in enumerate(pieces):
+            pairs = []
+            for a, b, lo, hi in pieces:
                 src = wides[s].at[pl.ds(start + a, b - a), pl.ds(lo, hi - lo)]
                 dst = wides[s].at[pl.ds(base(side) + a, b - a), pl.ds(lo, hi - lo)]
-                made.append(copy((name, s, side, n, chunk, k), src, dst, device))
-            return made
+                pairs.append((src, dst))
+            return parcel((name, s, side, n, chunk), pairs, device)
 
         def group(who, n):
             return who ^ 2 if n else who
@@ -495,30 +517,23 @@
             pieces = cut(sent(s, who, side, n), group(who, n), chunk)
             return boxes("xp", s, side, n, chunk, pieces, {"rep": me ^ 1}, base(side))
 
-        def extra_to_layer():
-            return boxes("e", "y", -1, 0, 0, cut(extra(me), me, (0, rows)), {"layer": before}, rows)
-
-        def extra_pass(who):
-            return boxes("ep", "y", -1, 0, 0, cut(extra(who), who, (0, rows)), {"rep": me ^ 1}, 2 * rows)
-
         def relay(s, chunk, who):
-            pieces = cut(relayed(who), who, chunk)
+            pieces = cut(shared(who), who, chunk)
             side = own_side(who)
             return boxes("r", s, side, 0, chunk, pieces, {"rep": me ^ 2}, base(side))
 
         def relay_pass(s, chunk, who):
-            pieces = cut(relayed(who), who, chunk)
+            pieces = cut(shared(who), who, chunk)
             side = own_side(who)
             return boxes("rp", s, side, 0, chunk, pieces, {"rep": me ^ 1}, base(side))
 
         def partial_out(s, chunk):
-            source, target = (z_out, z_in) if s == "z" else (y_out, y_in)
-            made = []
-            for k, (a, b, lo, hi) in enumerate(cut(own_spans(me), me, chunk)):
+            source, target = partials[s]
+            pairs = []
+            for a, b, lo, hi in cut(own_spans(me), me, chunk):
                 at = (pl.ds(a, b - a), pl.ds(lo - me * slots, hi - lo))
-                place = after if chip == 0 else before
-                made.append(copy(("p", s, chunk, k), source.at[at], target.at[at], {"layer": place}))
-            return made
+                pairs.append((source.at[at], target.at[at]))
+            return parcel(("p", s, chunk), pairs, {"layer": after if chip == 0 else before})
 
         def start_swap(s, chunk):
             begin(None, [swap(s, me, chunk)])
@@ -535,10 +550,7 @@
 
         def take_layer(s, n, chunk):
             for side in (1, -1):
-                onward = layer_pass(s, side, n, chunk, me)
-                if s != "y":
-                    onward = onward + relay(s, chunk, me)
-                take(may_take[side], to_layer(s, side, n, chunk), onward)
+                take(may_take[side], to_layer(s, side, n, chunk), layer_pass(s, side, n, chunk, me))
 
         def take_layer_pass(s, n, chunk):
             for side in (1, -1):
@@ -554,72 +566,95 @@
 
         for chunk in chunks:
             start_swap("y", chunk)
-            send_layer("y", 0, chunk)
-        for chunk in chunks:
-            start_pair("y", chunk)
-        yield
+        yield
+        for s in ("z", "y"):
+            for chunk in chunks:
+                send_layer(s, 0, chunk)
         for chunk in chunks:
             start_swap("z", chunk)
-        for chunk in chunks:
-            start_pair("z", chunk)
+        for s in ("y", "z"):
+            for chunk in chunks:
+                start_pair(s, chunk)
         for chunk in chunks:
             end_swap("y", chunk)
             send_layer("y", 1, chunk)
-        for n, chunk in enumerate(chunks):
-            take_layer("y", 0, chunk)
-        for n, chunk in enumerate(chunks):
+        for chunk in chunks:
+            take_layer("z", 0, chunk)
+        for chunk in chunks:
+            take(None, [pair("y", me ^ 1, chunk)])
+            take(None, [pass_pair("y", me ^ 3, chunk)])
+            take_layer_pass("z", 0, chunk)
+        yield
+        for chunk in chunks:
+            begin(may_send[out_side], partial_out("c", chunk))
+        for n, chunk in enumerate(chunks[:-1]):
             end_swap("z", chunk)
             take_layer("y", 1, chunk)
-        for chunk in chunks:
-            take(None, [pair("y", me ^ 1, chunk)])
-            take(None, [pass_pair("y", me ^ 3, chunk)])
             take(None, [pair("z", me ^ 1, chunk)])
-            for n in (0, 1):
-                take_layer_pass("y", n, chunk)
-        begin(may_send[-1], extra_to_layer())
-        for chunk in chunks:
-            send_layer("z", 0, chunk)
-        for chunk in chunks:
-            take(None, [pass_pair("z", me ^ 3, chunk)])
+            if n:
+                take(None, [pass_pair("z", me ^ 3, chunks[n - 1])])
+                yield
+        take_layer("y", 1, chunks[-1])
+        for chunk in chunks:
+            if chip == 1:
+                take_layer("y", 0, chunk)
+            take_layer_pass("y", 1, chunk)
+        if chip == 1:
+            for chunk in chunks:
+                take_layer_pass("y", 0, chunk)
+        take(None, [pair("z", me ^ 1, chunks[-1])])
+        take(None, [pass_pair("z", me ^ 3, chunks[-2])])
+        for chunk in chunks:
+            if chunk == chunks[-1]:
+                end_swap("z", chunk)
+                take(None, [pass_pair("z", me ^ 3, chunk)])
+            if chip == 0:
+                take_layer("y", 0, chunk)
+                take_layer_pass("y", 0, chunk)
+            take(may_take[out_side], partial_out("c", chunk))
             yield
             start_swap("u", chunk)
             start_pair("u", chunk)
+        for chunk in chunks:
             send_layer("u", 0, chunk)
-        take(may_take[-1], extra_to_layer(), extra_pass(me))
-        for n, chunk in enumerate(chunks):
-            take_layer("z", 0, chunk)
-            end_swap("u", chunk)
+        for chunk in chunks:
+            begin(may_take[own_side(me)], relay("z", chunk, me))
+        first, last = chunks[: len(chunks) // 2], chunks[len(chunks) // 2 :]
+        for some in (first, last):
+            for chunk in some:
+                if chunk != chunks[-1]:
+                    end_swap("u", chunk)
+                take_layer("u", 0, chunk)
+            for chunk in some:
+                take_layer_pass("u", 0, chunk)
+            yield
+        for chunk in chunks:
+            begin(may_send[out_side], partial_out("z", chunk))
+        for chunk in chunks[:: 1 if chip == 0 else -1]:
+            begin(may_take[own_side(me)], relay("u", chunk, me))
+        for chunk in chunks:
+            if chunk == chunks[-1]:
+                end_swap("u", chunk)
             take(None, [pair("u", me ^ 1, chunk)])
             take(None, [pass_pair("u", me ^ 3, chunk)])
+        yield
+        for chunk in chunks:
+            begin(may_send[out_side], partial_out("y", chunk))
+        yield
+        for chunk in chunks:
+            take_relay("z", chunk)
+        yield
+        for chunk in chunks:
+            take_relay_pass("z", chunk)
+        yield
+        arriving = chunks[:: 1 if chip == 1 else -1]
+        for chunk in arriving[:-1]:
+            take_relay("u", chunk)
+        for n, chunk in enumerate(arriving):
+            if n == len(arriving) - 2:
+                take_relay("u", arriving[-1])
+            take_relay_pass("u", chunk)
             yield
-        take(may_take[-1], extra_pass(me ^ 1))
-        for chunk in chunks[: len(chunks) // 2]:
-            take_layer("u", 0, chunk)
-        for chunk in chunks[: len(chunks) // 2]:
-            take_layer_pass("u", 0, chunk)
-        yield
-        for chunk in chunks[: len(chunks) // 2]:
-            begin(may_send[out_side], partial_out("z", chunk))
-        for chunk in chunks[len(chunks) // 2 :]:
-            take_layer("u", 0, chunk)
-        for chunk in chunks[len(chunks) // 2 :]:
-            take_layer_pass("u", 0, chunk)
-        yield
-        for chunk in chunks[len(chunks) // 2 :]:
-            begin(may_send[out_side], partial_out("z", chunk))
-        yield
-        for chunk in chunks:
-            begin(may_send[out_side], partial_out("y", chunk))
-        for chunk in chunks:
-            take_relay("z", chunk)
-        yield
-        for chunk in chunks:
-            take_layer_pass("z", 0, chunk)
-            take_relay("u", chunk)
-        for chunk in chunks:
-            take_relay_pass("z", chunk)
-            take_relay_pass("u", chunk)
-        yield
         for chunk in chunks:
             take(may_take[out_side], partial_out("z", chunk))
         yield
@@ -630,7 +665,7 @@
 
             def end(made=made):
                 for one in made:
-                    one().wait_send()
+                    one.wait_send()
 
             if made:
                 end() if guard is None else pl.when(guard)(end)
@@ -665,7 +700,7 @@
             rights.append(line)
         return multiply(lefts, rights)
 
-    def halo_part(i, left, right, inner):
+    def halo_part(i, left, right):
         lefts, rights = [], []
         for t in range(rows):
             u = lax.rem(t - i + band, band)
@@ -676,9 +711,8 @@
             for w in range(slots):
                 v = rep * slots + w + half - u
                 good = jnp.logical_and(inside, jnp.logical_and(v >= 0, v < band))
-                if inner:
-                    k = i - half + rep * slots + w
-                    good = jnp.logical_and(good, jnp.logical_and(k >= 0, k < rows))
+                k = i - half + rep * slots + w
+                good = jnp.logical_and(good, jnp.logical_and(k >= 0, k < rows))
                 line.append(jnp.where(good, right[i + u, lax.rem(v + band, band)], zero))
             rights.append(line)
         return multiply(lefts, rights)
@@ -686,11 +720,18 @@
     def split(total, w):
         return total[:, w * tile : (w + 1) * tile]
 
+    def returned(part, i, w):
+        k = i - half + rep * slots + w
+        below = jnp.logical_and(k < 0, layer > 0)
+        above = jnp.logical_and(k >= rows, layer + 1 < layers)
+        return jnp.where(jnp.logical_or(below, above), part[i, w].astype(jnp.float32), 0.0)
+
     def update_rows(chunk):
         def row(i, _):
-            total = own_part(i, z_wide, y_wide) + halo_part(i, z_wide, y_wide, False)
-            for w in range(slots):
-                value = -0.5 * split(total, w) + jnp.where(rep * slots + w == half, identity, 0.0)
+            total = halo_part(i, z_wide, y_wide)
+            for w in range(slots):
+                value = -0.5 * (split(total, w) + z_sum[i, w] + returned(c_in, i, w))
+                value += jnp.where(rep * slots + w == half, identity, 0.0)
                 value = jnp.where(pattern[i, w] == 1, value, 0.0)
                 u_wide[rows + i, rep * slots + w] = value.astype(jnp.bfloat16)
             return 0
@@ -706,14 +747,17 @@
 
         lax.fori_loop(chunk[0], chunk[1], row, 0)
 
-    def halo_rows(left, right, total):
-        def row(i, _):
-            value = halo_part(i, left, right, True)
+    def halo_rows(left, right, total, n, turn):
+        def row(r, _):
+            i = n * step + r
+            if turn:
+                i = lax.div(rep, 2) * (2 * n * step + step - rows) + rows - step - n * step + r
+            value = halo_part(i, left, right)
             for w in range(slots):
                 total[i, w] += split(value, w)
             return 0
 
-        lax.fori_loop(0, rows, row, 0)
+        lax.fori_loop(0, step if turn else rows, row, 0)
 
     def partial_rows(left, right, out, chunk):
         chip = lax.div(rep, 2)
@@ -738,11 +782,7 @@
     def finish(total, part, result):
         def row(i, _):
             for w in range(slots):
-                k = i - half + rep * slots + w
-                below = jnp.logical_and(k < 0, layer > 0)
-                above = jnp.logical_and(k >= rows, layer + 1 < layers)
-                more = jnp.where(jnp.logical_or(below, above), part[i, w].astype(jnp.float32), 0.0)
-                value = jnp.where(pattern[i, w] == 1, total[i, w] + more, 0.0)
+                value = jnp.where(pattern[i, w] == 1, total[i, w] + returned(part, i, w), 0.0)
                 result[i, w] = value.astype(jnp.bfloat16)
             return 0
 
@@ -752,24 +792,33 @@
     pl.semaphore_wait(barrier, 4)
     advance()
     keep(z_own, z_wide)
+    middle = rows // 2
+    advance()
+    partial_rows(z_wide, y_wide, c_out, (0, rows))
+    for chunk in chunks[:-2]:
+        advance()
+        own_rows(z_wide, y_wide, z_sum, chunk)
     for chunk in chunks:
         advance()
+        if chunk == chunks[0]:
+            own_rows(z_wide, y_wide, z_sum, chunks[-2])
+        if chunk == chunks[-1]:
+            own_rows(z_wide, y_wide, z_sum, chunk)
         update_rows(chunk)
-    for chunk in chunks:
+    for chunk in ((0, middle), (middle, rows)):
         advance()
-        own_rows(u_wide, z_wide, z_sum, chunk)
-    advance()
-    middle = rows // 2
-    partial_rows(u_wide, z_wide, z_out, (0, middle))
-    advance()
-    partial_rows(u_wide, z_wide, z_out, (middle, rows))
+        partial_rows(u_wide, z_wide, z_out, chunk)
     advance()
     partial_rows(y_wide, u_wide, y_out, (0, rows))
     advance()
+    own_rows(u_wide, z_wide, z_sum, (0, rows))
+    advance()
     own_rows(y_wide, u_wide, y_sum, (0, rows))
     advance()
-    halo_rows(u_wide, z_wide, z_sum)
-    halo_rows(y_wide, u_wide, y_sum)
+    halo_rows(u_wide, z_wide, z_sum, 0, False)
+    for n in range(len(chunks)):
+        advance()
+        halo_rows(y_wide, u_wide, y_sum, n, True)
     advance()
     finish(z_sum, z_in, z_next)
     advance()
@@ -792,7 +841,7 @@
         if paired:
             kernel = paired_kernel
             extra = [pltpu.VMEM((rows, slots) + tile, jnp.float32)] * 2
-            extra += [pltpu.VMEM((rows, slots) + tile, jnp.bfloat16)] * 4
+            extra += [pltpu.VMEM((rows, slots) + tile, jnp.bfloat16)] * 6
             sems = [pltpu.SemaphoreType.DMA((1,)), pltpu.SemaphoreType.DMA((PAIRED_SEMAPHORES,))]
         return pl.pallas_call(
             functools.partial(kernel, layers, reps, (rows, slots, tile[0])),
@@ -801,7 +850,7 @@
             out_specs=(VMEM, VMEM),
             scratch_shapes=[wide, wide, wide] + extra + sems,
             compiler_params=pltpu.CompilerParams(
-                collective_id=0, has_side_effects=True, vmem_limit_bytes=60 * 1024 * 1024
+                collective_id=0, has_side_effects=True, vmem_limit_bytes=VMEM_BYTES if paired else 60 * 1024 * 1024
             ),
             name="newton_step",
         )(pattern, inverse_root, square_root)

time: 120 us -> 112 us (0.933)
  the two profiles are of different devices: /device:TPU:2 before, /device:TPU:10 now
where the time goes in v2:
time: 112 us
  Pallas kernels  108 us (96%)
  local copies, waits for them, and re-layouts  3.32 us (3%)
    pallas_call x1, Pallas kernels, body(): pl.pallas_call(functools.partial(kernel, layers, reps, (rows, slots, tile...  108 us
    unnamed x5, local copies, waits for them, and re-layouts  3.32 us

profile of v2, /device:TPU:10, one launch (start us, length us, event | category | flops | bytes accessed | tf_op | source)
XLA Modules:
  0.0 112.1 jit_solution(6260741562555370878)
XLA Ops:
  0.6 0.8 copy.5.pattern
  1.4 108.1 %newton_step.1 = (bf16[8,4,128,128]{3,2,1,0:T(8,128)(2,1)S(1)}, bf16[8,4,128,128]{3,2,1,0:T(8,128)(2,1)}) custom-call(s32[8,4]{1,0:T(8,128)S(1)} %copy.5.pattern, bf16[8,4,128,128]{3,2,1,0:T(8,128)(2,1)} %z_own.1, bf16[8,4,128,128]{3,2,1,0:T(8,128)(2,1)} %y_own.1), custom_call_target="tpu_custom_call" | custom-call | tf_op jit(solution)/shard_map/newton_step/pallas_call | solution.py:846
  109.5 0.0 copy-start
  109.5 1.0 copy.8
  110.5 0.6 copy-done
  111.1 1.0 copy.9
Async XLA Ops:
  109.5 1.6 %copy-start = (bf16[8,4,128,128]{3,2,1,0:T(8,128)(2,1)S(1)}, bf16[8,4,128,128]{3,2,1,0:T(8,128)(2,1)}, u32[]{:S(2)}) copy-start(bf16[8,4,128,128]{3,2,1,0:T(8,128)(2,1)} %get-tuple-element.5) | copy-start | bytes 3145732

commit v3 on v2

--- a/solution.py
+++ b/solution.py
@@ -346,7 +346,7 @@
 
 
 PAIRED_SEMAPHORES = 144
-VMEM_BYTES = 52 * 1024 * 1024
+VMEM_BYTES = 50 * 1024 * 1024
 
 
 def block_spans(rows, band):
@@ -605,8 +605,9 @@
         take(None, [pair("z", me ^ 1, chunks[-1])])
         take(None, [pass_pair("z", me ^ 3, chunks[-2])])
         for chunk in chunks:
+            if chunk == chunks[1]:
+                end_swap("z", chunks[-1])
             if chunk == chunks[-1]:
-                end_swap("z", chunk)
                 take(None, [pass_pair("z", me ^ 3, chunk)])
             if chip == 0:
                 take_layer("y", 0, chunk)
@@ -615,8 +616,10 @@
             yield
             start_swap("u", chunk)
             start_pair("u", chunk)
-        for chunk in chunks:
-            send_layer("u", 0, chunk)
+            if chunk == chunks[-2]:
+                for one in chunks[:-1]:
+                    send_layer("u", 0, one)
+        send_layer("u", 0, chunks[-1])
         for chunk in chunks:
             begin(may_take[own_side(me)], relay("z", chunk, me))
         first, last = chunks[: len(chunks) // 2], chunks[len(chunks) // 2 :]

time: 112 us -> 109 us (0.973)
  the two profiles are of different devices: /device:TPU:10 before, /device:TPU:5 now
where the time goes in v3:
time: 109 us
  Pallas kernels  104 us (95%)
  local copies, waits for them, and re-layouts  3.92 us (4%)
    pallas_call x1, Pallas kernels, body(): pl.pallas_call(functools.partial(kernel, layers, reps, (rows, slots, tile...  104 us
    unnamed x5, local copies, waits for them, and re-layouts  3.92 us

profile of v3, /device:TPU:5, one launch (start us, length us, event | category | flops | bytes accessed | tf_op | source)
XLA Modules:
  0.0 108.8 jit_solution(5649239985626721970)
XLA Ops:
  0.6 0.8 copy.5.pattern
  1.4 0.0 copy-start
  1.4 1.2 %copy-done = bf16[8,4,128,128]{3,2,1,0:T(8,128)(2,1)S(1)} copy-done((bf16[8,4,128,128]{3,2,1,0:T(8,128)(2,1)S(1)}, bf16[8,4,128,128]{3,2,1,0:T(8,128)(2,1)}, u32[]{:S(2)}) %copy-start) | copy-done | bytes 1048600
  2.6 104.2 %newton_step.1 = (bf16[8,4,128,128]{3,2,1,0:T(8,128)(2,1)S(1)}, bf16[8,4,128,128]{3,2,1,0:T(8,128)(2,1)S(1)}) custom-call(s32[8,4]{1,0:T(8,128)S(1)} %copy.5.pattern, bf16[8,4,128,128]{3,2,1,0:T(8,128)(2,1)S(1)} %copy-done, bf16[8,4,128,128]{3,2,1,0:T(8,128)(2,1)} %y_own.1), custom_call_target="tpu_custom_call" | custom-call | tf_op jit(solution)/shard_map/newton_step/pallas_call | solution.py:849
  106.8 1.0 copy.8
  107.8 1.0 copy.9
Async XLA Ops:
  1.4 1.2 %copy-start = (bf16[8,4,128,128]{3,2,1,0:T(8,128)(2,1)S(1)}, bf16[8,4,128,128]{3,2,1,0:T(8,128)(2,1)}, u32[]{:S(2)}) copy-start(bf16[8,4,128,128]{3,2,1,0:T(8,128)(2,1)} %z_own.1) | copy-start | bytes 3145732

commit v4 on v3

--- a/solution.py
+++ b/solution.py
@@ -345,7 +345,7 @@
     return total
 
 
-PAIRED_SEMAPHORES = 144
+PAIRED_SEMAPHORES = 152
 VMEM_BYTES = 50 * 1024 * 1024
 
 
@@ -440,7 +440,7 @@
         def sent(s, who, side, n):
             if side == own_side(who):
                 return {} if n else own_spans(who)
-            return shared(who ^ 2) if n and s == "y" else {}
+            return shared(who ^ 2) if n and (s == "y" or s == "z" and who // 2) else {}
 
         def shared(who):
             side = own_side(who)
@@ -518,12 +518,12 @@
             return boxes("xp", s, side, n, chunk, pieces, {"rep": me ^ 1}, base(side))
 
         def relay(s, chunk, who):
-            pieces = cut(shared(who), who, chunk)
+            pieces = cut(shared(who), who, chunk) if s == "u" or who // 2 else []
             side = own_side(who)
             return boxes("r", s, side, 0, chunk, pieces, {"rep": me ^ 2}, base(side))
 
         def relay_pass(s, chunk, who):
-            pieces = cut(shared(who), who, chunk)
+            pieces = cut(shared(who), who, chunk) if s == "u" or who // 2 else []
             side = own_side(who)
             return boxes("rp", s, side, 0, chunk, pieces, {"rep": me ^ 1}, base(side))
 
@@ -607,6 +607,8 @@
         for chunk in chunks:
             if chunk == chunks[1]:
                 end_swap("z", chunks[-1])
+                for one in chunks:
+                    send_layer("z", 1, one)
             if chunk == chunks[-1]:
                 take(None, [pass_pair("z", me ^ 3, chunk)])
             if chip == 0:
@@ -646,21 +648,23 @@
         yield
         for chunk in chunks:
             take_relay("z", chunk)
+            take_layer("z", 1, chunk)
         yield
         for chunk in chunks:
             take_relay_pass("z", chunk)
+            take_layer_pass("z", 1, chunk)
         yield
         arriving = chunks[:: 1 if chip == 1 else -1]
-        for chunk in arriving[:-1]:
+        for chunk in arriving[:2]:
             take_relay("u", chunk)
+        for chunk in chunks:
+            take(may_take[out_side], partial_out("z", chunk))
+        yield
         for n, chunk in enumerate(arriving):
-            if n == len(arriving) - 2:
-                take_relay("u", arriving[-1])
+            for one in arriving[n + 1 : n + 2] if n else ():
+                take_relay("u", one)
             take_relay_pass("u", chunk)
             yield
-        for chunk in chunks:
-            take(may_take[out_side], partial_out("z", chunk))
-        yield
         for chunk in chunks:
             take(may_take[out_side], partial_out("y", chunk))
         yield
@@ -819,11 +823,11 @@
     own_rows(y_wide, u_wide, y_sum, (0, rows))
     advance()
     halo_rows(u_wide, z_wide, z_sum, 0, False)
+    advance()
+    finish(z_sum, z_in, z_next)
     for n in range(len(chunks)):
         advance()
         halo_rows(y_wide, u_wide, y_sum, n, True)
-    advance()
-    finish(z_sum, z_in, z_next)
     advance()
     finish(y_sum, y_in, y_next)
     advance()

time: 109 us -> 107 us (0.982)
  the two profiles are of different devices: /device:TPU:5 before, /device:TPU:10 now
where the time goes in v4:
time: 107 us
  Pallas kernels  102 us (95%)
  local copies, waits for them, and re-layouts  3.92 us (4%)
    pallas_call x1, Pallas kernels, body(): pl.pallas_call(functools.partial(kernel, layers, reps, (rows, slots, tile...  102 us
    unnamed x5, local copies, waits for them, and re-layouts  3.92 us

profile of v4, /device:TPU:10, one launch (start us, length us, event | category | flops | bytes accessed | tf_op | source)
XLA Modules:
  0.0 106.8 jit_solution(7314340091232858540)
XLA Ops:
  0.6 0.8 copy.5.pattern
  1.4 0.0 copy-start
  1.4 1.2 %copy-done = bf16[8,4,128,128]{3,2,1,0:T(8,128)(2,1)S(1)} copy-done((bf16[8,4,128,128]{3,2,1,0:T(8,128)(2,1)S(1)}, bf16[8,4,128,128]{3,2,1,0:T(8,128)(2,1)}, u32[]{:S(2)}) %copy-start) | copy-done | bytes 1048600
  2.6 102.3 %newton_step.1 = (bf16[8,4,128,128]{3,2,1,0:T(8,128)(2,1)S(1)}, bf16[8,4,128,128]{3,2,1,0:T(8,128)(2,1)S(1)}) custom-call(s32[8,4]{1,0:T(8,128)S(1)} %copy.5.pattern, bf16[8,4,128,128]{3,2,1,0:T(8,128)(2,1)S(1)} %copy-done, bf16[8,4,128,128]{3,2,1,0:T(8,128)(2,1)} %y_own.1), custom_call_target="tpu_custom_call" | custom-call | tf_op jit(solution)/shard_map/newton_step/pallas_call | solution.py:853
  104.9 1.0 copy.8
  105.8 1.0 copy.9
Async XLA Ops:
  1.4 1.2 %copy-start = (bf16[8,4,128,128]{3,2,1,0:T(8,128)(2,1)S(1)}, bf16[8,4,128,128]{3,2,1,0:T(8,128)(2,1)}, u32[]{:S(2)}) copy-start(bf16[8,4,128,128]{3,2,1,0:T(8,128)(2,1)} %z_own.1) | copy-start | bytes 3145732
